TPU v7x, 32 devices: a whole 2x2x4 slice. The times are simulated.
32 devices in a mesh: copy: 2 (over core), fsdp: 4 (over z), tp: 4 (over y, x).
Axes of the slice: x: 2, y: 2, z: 4, core: 2. Of those that a mesh axis runs over, the one named last changes fastest.
Arguments:
- gradients: float32 [32, 128, 4096], P('copy', 'fsdp', 'tp'), parts along dimension 0, may hold values from -6 to 6
- momentum: float32 [32, 128, 4096], P('copy', 'fsdp', 'tp'), parts along dimension 0, may hold values from -6 to 6
- weights: float32 [32, 128, 4096], P('copy', 'fsdp', 'tp'), parts along dimension 0, may hold values from -0.1875 to 0.1875
Outputs:
- new_weights: float32 [32, 128, 4096], P('copy', 'fsdp', 'tp'), parts along dimension 0
- new_momentum: float32 [32, 128, 4096], P('copy', 'fsdp', 'tp'), parts along dimension 0
There are 2 independent parts, one for each index of `copy`. A program takes and returns all parts, laid end to end along the dimension named above; each array names one. Nothing has to cross between parts.
All inputs are finite; a program needn't handle non-finite values.
Results may differ from a plain program's by a relative error of at most 0.00014.
Values sent between devices are 32-bit elements; how exact they have to be, the bound alone decides.
A program may use at most 64 MiB of HBM per device.

v0:
```python
import jax
import jax.numpy as jnp
from jax import lax
from jax.sharding import PartitionSpec as P

ITERS = 4


hold_rate = 0.95
learn_rate = 0.9
decay_rate = 0.1


def shards(gradients, momentum, weights):
    new_momentum = hold_rate * momentum + gradients
    direction = hold_rate * new_momentum + gradients
    moved = lax.all_to_all(direction, "fsdp", split_axis=0, concat_axis=1, tiled=True)
    whole = lax.all_to_all(moved, "tp", split_axis=0, concat_axis=2, tiled=True)
    iterate = whole * lax.rsqrt(jnp.sum(whole * whole, axis=(1, 2), keepdims=True) + 1e-06)
    for step in range(ITERS):
        gram = jnp.einsum("mik,mjk->mij", iterate, iterate, precision=lax.Precision.HIGHEST)
        mixed = -4.775 * gram + 2.0315 * jnp.einsum(
            "mij,mjk->mik", gram, gram, precision=lax.Precision.HIGHEST
        )
        iterate = 3.4445 * iterate + jnp.einsum(
            "mij,mjk->mik", mixed, iterate, precision=lax.Precision.HIGHEST
        )
    iterate = lax.all_to_all(iterate, "tp", split_axis=2, concat_axis=0, tiled=True)
    back = lax.all_to_all(iterate, "fsdp", split_axis=1, concat_axis=0, tiled=True)
    new_weights = (1.0 - learn_rate * decay_rate) * weights - learn_rate * back
    return (new_weights, new_momentum)


def solution(mesh):
    return jax.shard_map(
        shards,
        mesh=mesh,
        in_specs=(P("copy", "fsdp", "tp"), P("copy", "fsdp", "tp"), P("copy", "fsdp", "tp")),
        out_specs=(P("copy", "fsdp", "tp"), P("copy", "fsdp", "tp")),
        check_vma=False,
    )
```

profile of v0, /device:TPU:0, one launch (start us, length us, event | category | flops | bytes accessed | tf_op | source)
XLA Modules:
  0.0 203.1 jit_solution(4223849455664191840)
XLA Ops:
  0.6 4.3 %multiply_add_fusion = (f32[16,32,1024]{2,1,0:T(8,128)S(1)}, f32[16,32,1024]{2,1,0:T(8,128)}) fusion(f32[16,32,1024]{2,1,0:T(8,128)} %param.3, f32[16,32,1024]{2,1,0:T(8,128)} %param.4), kind=kLoop, calls=%fused_computation.11 | loop fusion | flops 2097152 | bytes 8388608 | tf_op jit(solution)/shard_map/add | solution.py:16
  4.9 54.3 %all_to_all.54 = f32[16,32,1024]{2,1,0:T(8,128)S(1)} all-to-all(f32[16,32,1024]{2,1,0:T(8,128)S(1)} %get-tuple-element.2), channel_id=1, replica_groups=mesh['copy'=2,'fsdp'=4,'tp'=4] {'fsdp'}, dimensions={0} | all-to-all | bytes 4194304 | tf_op jit(solution)/shard_map/all_to_all | solution.py:17
  59.2 0.2 copy.30
  59.5 27.8 %all_to_all.55 = f32[4,128,1024]{2,1,0:T(8,128)S(1)} all-to-all(f32[4,128,1024]{2,1,0:T(8,128)S(1)} %bitcast.58), channel_id=1, replica_groups=mesh['copy'=2,'fsdp'=4,'tp'=4] {'tp'}, dimensions={0} | all-to-all | bytes 4194304 | tf_op jit(solution)/shard_map/all_to_all | solution.py:18
  87.3 1.1 multiply_reduce_fusion
  89.1 1.8 fusion.4
  90.9 0.2 fusion.10
  91.1 2.6 %multiply_bitcast_fusion.1 = (f32[1,128,4,1024]{3,1,2,0:T(8,128)}, f32[1,128,4,1024]{3,1,2,0:T(8,128)}) fusion(f32[4,128,1024]{2,1,0:T(8,128)S(1)} %all_to_all.55, f32[]{:T(128)S(6)} %rsqrt.4), kind=kLoop, calls=%fused_computation.14 | loop fusion | flops 1048576 | bytes 6291460 | tf_op jit(solution)/shard_map/mul | solution.py:19
  93.7 1.9 copy.32
  95.6 2.9 %copy.31 = f32[1,128,4,1024]{1,3,2,0:T(8,128)} copy(f32[1,128,4,1024]{3,1,2,0:T(8,128)} %get-tuple-element.5) | data formatting | bytes 4194304 | tf_op jit(solution)/shard_map/mul | solution.py:25
  98.5 3.0 %copy.33 = f32[128,4096]{1,0:T(8,128)} copy(f32[128,4096]{0,1:T(8,128)} %bitcast.59) | data formatting | bytes 4194304 | tf_op jit(solution)/shard_map/mul | solution.py:25
  101.4 3.6 %convolution_add_fusion.3 = f32[128,4096]{1,0:T(8,128)S(1)} fusion(f32[128,4096]{1,0:T(8,128)} %copy.33, f32[128,128]{1,0:T(8,128)S(1)} %fusion.10, f32[128,4096]{0,1:T(8,128)S(1)} %bitcast.56), kind=kOutput, calls=%fused_computation.4 | convolution fusion | flops 805830656 | bytes 6356992 | tf_op jit(solution)/shard_map/mij,mjk->mik/dot_general | solution.py:25
  105.0 1.8 fusion.12
  106.8 0.2 fusion.9
  107.0 2.0 %convolution_add_fusion.2 = f32[128,4096]{1,0:T(8,128)S(1)} fusion(f32[128,128]{1,0:T(8,128)S(1)} %fusion.9, f32[128,4096]{1,0:T(8,128)S(1)} %convolution_add_fusion.3), kind=kOutput, calls=%fused_computation.3 | convolution fusion | flops 806354944 | bytes 4259840 | tf_op jit(solution)/shard_map/mij,mjk->mik/dot_general | solution.py:25
  109.1 1.8 fusion.13
  110.9 0.2 fusion.8
  111.1 2.0 %convolution_add_fusion.1 = f32[128,4096]{1,0:T(8,128)S(1)} fusion(f32[128,128]{1,0:T(8,128)S(1)} %fusion.8, f32[128,4096]{1,0:T(8,128)S(1)} %convolution_add_fusion.2), kind=kOutput, calls=%fused_computation.2 | convolution fusion | flops 806354944 | bytes 4259840 | tf_op jit(solution)/shard_map/mij,mjk->mik/dot_general | solution.py:25
  113.2 1.8 fusion.14
  115.0 0.2 fusion.7
  115.2 2.3 %fusion = f32[1,128,4096]{2,1,0:T(8,128)S(1)} fusion(f32[128,128]{1,0:T(8,128)S(1)} %fusion.7, f32[128,4096]{1,0:T(8,128)S(1)} %convolution_add_fusion.1), kind=kOutput, calls=%fused_computation.1 | convolution fusion | flops 806354944 | bytes 4259840 | tf_op jit(solution)/shard_map/mij,mjk->mik/dot_general | solution.py:25
  117.5 3.7 %copy.34 = f32[1,128,4096]{1,0,2:T(1,128)} copy(f32[1,128,4096]{2,1,0:T(8,128)S(1)} %fusion) | data formatting | bytes 4194304 | tf_op jit(solution)/shard_map/add | solution.py:25
  121.2 26.5 %all_to_all.56 = f32[1,128,4096]{1,0,2:T(1,128)S(1)} all-to-all(f32[1,128,4096]{1,0,2:T(1,128)} %copy.34), channel_id=1, replica_groups=mesh['copy'=2,'fsdp'=4,'tp'=4] {'tp'}, dimensions={2} | all-to-all | bytes 4194304 | tf_op jit(solution)/shard_map/all_to_all | solution.py:28
  147.6 2.0 copy.35
  149.6 48.8 %all_to_all.57 = f32[4,128,1024]{2,0,1:T(4,128)S(1)} all-to-all(f32[4,128,1024]{2,0,1:T(4,128)} %copy.35), channel_id=1, replica_groups=mesh['copy'=2,'fsdp'=4,'tp'=4] {'fsdp'}, dimensions={1} | all-to-all | bytes 4194304 | tf_op jit(solution)/shard_map/all_to_all | solution.py:29
  198.4 1.4 copy_multiply_fusion
  199.8 0.0 copy-start
  199.8 0.2 copy.37
  200.0 1.3 copy-done
  201.4 1.8 bitcast_subtract_fusion
Async XLA Ops:
  199.8 1.6 copy-start
where the time goes:
time: 204 us; the launch traced here: 203 us
  blocking collectives  157 us (77%)
  matrix products  17.9 us (9%)
  local copies, waits for them, and re-layouts  15.2 us (7%)
  other arithmetic  11.1 us (5%)
    all_to_all x1, blocking collectives, shards(): lax.all_to_all(direction, 'fsdp', split_axis=0, concat_axis=1, tiled=True)  54.3 us
    all_to_all x1, blocking collectives, shards(): lax.all_to_all(iterate, 'fsdp', split_axis=1, concat_axis=0, tiled=True)  48.8 us
    all_to_all x1, blocking collectives, shards(): whole = lax.all_to_all(moved, 'tp', split_axis=0, concat_axis=2, tiled=True)  27.8 us
    all_to_all x1, blocking collectives, shards(): lax.all_to_all(iterate, 'tp', split_axis=2, concat_axis=0, tiled=True)  26.5 us
    dot_general x4, matrix products, shards(): jnp.einsum('mij,mjk->mik', mixed, iterate, precision=lax.Precision.HIGHEST)  9.94 us
    dot_general x4, matrix products, shards(): jnp.einsum('mik,mjk->mij', iterate, iterate, precision=lax.Precision.HIGH...  7.16 us
    mul x2, local copies, waits for them, and re-layouts, shards(): 3.4445 * iterate  5.84 us
    add x1, other arithmetic, shards(): direction = hold_rate * new_momentum + gradients  4.27 us

commit v1 on v0

v1 whole, which is shorter than its diff:
```python
import jax
import jax.numpy as jnp
from jax import lax
from jax.sharding import PartitionSpec as P

ITERS = 4


hold_rate = 0.95
learn_rate = 0.9
decay_rate = 0.1


def mul(a, b):
    return jnp.einsum("mij,mjk->mik", a, b, precision=lax.Precision.HIGHEST)


def mixing(gram):
    eye = jnp.eye(gram.shape[-1], dtype=gram.dtype)
    scale = lax.rsqrt(jnp.sum(gram * eye, axis=(1, 2), keepdims=True) + 1e-06)
    gram = gram * scale * scale
    total = scale * eye
    for step in range(ITERS):
        poly = 3.4445 * eye - 4.775 * gram + 2.0315 * mul(gram, gram)
        total = mul(poly, total)
        if step < ITERS - 1:
            gram = mul(poly, mul(gram, poly))
    return total


def shards(gradients, momentum, weights):
    new_momentum = hold_rate * momentum + gradients
    direction = hold_rate * new_momentum + gradients
    moved = lax.all_to_all(direction, "fsdp", split_axis=0, concat_axis=1, tiled=True)
    gram = jnp.einsum("mik,mjk->mij", moved, moved, precision=lax.Precision.HIGHEST)
    gram = lax.psum(gram, "tp")
    iterate = mul(mixing(gram), moved)
    back = lax.all_to_all(iterate, "fsdp", split_axis=1, concat_axis=0, tiled=True)
    new_weights = (1.0 - learn_rate * decay_rate) * weights - learn_rate * back
    return (new_weights, new_momentum)


def solution(mesh):
    return jax.shard_map(
        shards,
        mesh=mesh,
        in_specs=(P("copy", "fsdp", "tp"), P("copy", "fsdp", "tp"), P("copy", "fsdp", "tp")),
        out_specs=(P("copy", "fsdp", "tp"), P("copy", "fsdp", "tp")),
        check_vma=False,
    )
```

time: 204 us -> 187 us (0.917)
  blocking collectives: 157 us -> 106 us
  waiting for transfers between devices: 0 us -> 42.4 us
  between operations: 1.45 us -> 14.2 us
  local copies, waits for them, and re-layouts: 15.2 us -> 3.07 us
  matrix products: 17.9 us -> 12.4 us
  other arithmetic: 11.1 us -> 7.95 us
    all_to_all x2 -> x0, blocking collectives: 54.3 us -> none  [the longest x1 27.8 us: shards(): whole = lax.all_to_all(moved, 'tp', split_axis=0, concat_axis=2, tiled=True)]
    psum x0 -> x1, waiting for transfers between devices: none -> 42.4 us  [shards(): gram = lax.psum(gram, 'tp')]
    mul x3 -> x0, local copies, waits for them, and re-layouts: 7.74 us -> none  [the longest x2 5.84 us: shards(): 3.4445 * iterate]
    dot_general x12 -> x16, matrix products: 17.9 us -> 12.4 us  [the longest x15 9.65 us: mul(): return jnp.einsum('mij,mjk->mik', a, b, precision=lax.Precision.HIGHEST)]
    add x1 -> x0, local copies, waits for them, and re-layouts: 3.7 us -> none  [shards(): 3.4445 * iterate]
    all_to_all x1, blocking collectives: 48.8 us -> 52.1 us  [shards(): lax.all_to_all(iterate, 'fsdp', split_axis=1, concat_axis=0, tiled=True)]
    mul x1, other arithmetic: 2.56 us -> 0.01 us  [mixing(): poly = 3.4445 * eye - 4.775 * gram + 2.0315 * mul(gram, gram)]
  transfers between devices with their start and end apart: 0 -> 1, of which waited for: 0 -> 1; matrix products, arithmetic and copies ran while one was open for 0% -> 0% of each run, Pallas kernels for 0% -> 0%
where the time goes in v1:
time: 187 us
  blocking collectives  106 us (57%)
  waiting for transfers between devices  42.4 us (23%)
  between operations  14.2 us (8%)
  matrix products  12.4 us (7%)
  other arithmetic  7.95 us (4%)
  local copies, waits for them, and re-layouts  3.07 us (2%)
    all_to_all x1, blocking collectives, shards(): lax.all_to_all(direction, 'fsdp', split_axis=0, concat_axis=1, tiled=True)  54.3 us
    all_to_all x1, blocking collectives, shards(): lax.all_to_all(iterate, 'fsdp', split_axis=1, concat_axis=0, tiled=True)  52.1 us
    psum x1, waiting for transfers between devices, shards(): gram = lax.psum(gram, 'tp')  42.4 us
    dot_general x15, matrix products, mul(): return jnp.einsum('mij,mjk->mik', a, b, precision=lax.Precision.HIGHEST)  9.65 us
    add x1, other arithmetic, shards(): direction = hold_rate * new_momentum + gradients  4.5 us
  transfers between devices with their start and end apart: 1, of which 1 were waited for; matrix products, arithmetic and copies ran while one was open for 0% of the time, Pallas kernels for 0%

profile of v1, /device:TPU:0, one launch (start us, length us, event | category | flops | bytes accessed | tf_op | source)
XLA Modules:
  0.0 186.5 jit_solution(14155956798188366832)
XLA Ops:
  7.2 0.0 all-reduce.2.cloned.1.call-start
  7.2 4.5 %multiply_add_fusion = (f32[16,32,1024]{2,1,0:T(8,128)S(1)}, f32[16,32,1024]{2,1,0:T(8,128)}) fusion(f32[16,32,1024]{2,1,0:T(8,128)} %param.3, f32[16,32,1024]{2,1,0:T(8,128)} %param.4), kind=kLoop, calls=%fused_computation.1 | loop fusion | flops 2097152 | bytes 8388608 | tf_op jit(solution)/shard_map/add | solution.py:33
  11.7 54.3 %all_to_all.27 = f32[16,32,1024]{2,1,0:T(8,128)S(1)} all-to-all(f32[16,32,1024]{2,1,0:T(8,128)S(1)} %get-tuple-element.2), channel_id=1, replica_groups=mesh['copy'=2,'fsdp'=4,'tp'=4] {'fsdp'}, dimensions={0} | all-to-all | bytes 4194304 | tf_op jit(solution)/shard_map/all_to_all | solution.py:34
  66.0 0.1 copy.7
  66.2 2.8 %fusion.13 = f32[4,128,128]{2,1,0:T(8,128)} fusion(f32[4,128,1024]{2,1,0:T(8,128)S(1)} %bitcast.37), kind=kOutput, calls=%fused_computation.25 | convolution fusion | flops 805306368 | bytes 2359296 | tf_op jit(solution)/shard_map/mik,mjk->mij/dot_general | solution.py:35
  68.9 0.0 all-reduce.2.cloned.1.call-update
  69.0 42.4 %all-reduce.2.cloned.1.call-done = f32[4,128,128]{2,1,0:T(8,128)} async-done(((f32[4,128,128]{2,1,0:T(8,128)}), f32[4,128,128]{2,1,0:T(8,128)}) %all-reduce.2.cloned.1.call-update) | async-done | bytes 262160 | tf_op jit(solution)/shard_map/psum | solution.py:36
  111.4 1.1 multiply_reduce_fusion
  112.5 1.6 fusion.3
  114.1 0.4 fusion.4
  114.6 1.4 fusion.6
  116.0 0.4 fusion.14
  116.4 0.4 fusion.2
  116.7 0.4 fusion.15
  117.1 0.4 fusion.19
  117.5 0.4 fusion.16
  118.0 0.4 fusion.1
  118.3 0.4 fusion.17
  118.7 0.4 fusion.20
  119.1 0.4 fusion.18
  119.5 0.4 fusion
  119.9 0.4 fusion.21
  120.3 1.9 %fusion.22 = f32[4,128,1024]{2,1,0:T(8,128)S(1)} fusion(f32[4,128,128]{2,1,0:T(8,128)S(1)} %fusion.21, f32[4,128,1024]{2,1,0:T(8,128)S(1)} %bitcast.38), kind=kOutput, calls=%fused_computation.34 | convolution fusion | flops 805306368 | bytes 4456448 | tf_op jit(solution)/shard_map/mij,mjk->mik/dot_general | solution.py:15
  122.3 1.4 copy.8
  123.6 52.1 %all_to_all.28 = f32[4,128,1024]{2,0,1:T(4,128)S(1)} all-to-all(f32[4,128,1024]{2,0,1:T(4,128)S(1)} %copy.8), channel_id=1, replica_groups=mesh['copy'=2,'fsdp'=4,'tp'=4] {'fsdp'}, dimensions={1} | all-to-all | bytes 4194304 | tf_op jit(solution)/shard_map/all_to_all | solution.py:38
  175.7 0.6 broadcast_multiply_fusion
  176.3 0.0 copy-start
  176.3 1.2 copy.9
  177.6 0.4 copy-done
  177.9 1.8 bitcast_subtract_fusion
  (3 shorter events, 0.0 us)
Async XLA Ops:
  7.2 104.2 %all-reduce.2.cloned.1.call-start = ((), (), s32[]{:S(2)}) async-start(), calls=%async_computation.2 | async-start | bytes 524288 | tf_op jit(solution)/shard_map/psum | solution.py:36
  176.3 1.6 copy-start
Sparse Core Ops, SparseCore 0:
  69.1 42.2 all-reduce.1

commit v2 on v1

v2 whole, which is shorter than its diff:
```python
import functools

import jax
import jax.numpy as jnp
from jax import lax
from jax.experimental import pallas as pl
from jax.experimental.pallas import tpu as pltpu
from jax.sharding import PartitionSpec as P

ITERS = 4


hold_rate = 0.95
learn_rate = 0.9
decay_rate = 0.1

MESH = pl.DeviceIdType.MESH


def dot(a, b, contract=((1,), (0,))):
    return lax.dot_general(
        a,
        b,
        (contract, ((), ())),
        precision=lax.Precision.HIGHEST,
        preferred_element_type=jnp.float32,
    )


def mixing(gram):
    side = gram.shape[0]
    eye = (
        lax.broadcasted_iota(jnp.int32, (side, side), 0)
        == lax.broadcasted_iota(jnp.int32, (side, side), 1)
    ).astype(jnp.float32)
    scale = lax.rsqrt(jnp.sum(gram * eye, keepdims=True) + 1e-06)
    gram = gram * scale * scale
    total = scale * eye
    for step in range(ITERS):
        poly = 3.4445 * eye - 4.775 * gram + 2.0315 * dot(gram, gram)
        total = poly * scale if step == 0 else dot(poly, total)
        if step < ITERS - 1:
            gram = dot(poly, dot(gram, poly))
    return total


def plain(gradients, momentum, weights):
    new_momentum = hold_rate * momentum + gradients
    direction = hold_rate * new_momentum + gradients
    moved = lax.all_to_all(direction, "fsdp", split_axis=0, concat_axis=1, tiled=True)
    gram = jnp.einsum("mik,mjk->mij", moved, moved, precision=lax.Precision.HIGHEST)
    gram = lax.psum(gram, "tp")
    mixed = jax.vmap(mixing)(gram)
    iterate = jnp.einsum("mij,mjk->mik", mixed, moved, precision=lax.Precision.HIGHEST)
    back = lax.all_to_all(iterate, "fsdp", split_axis=1, concat_axis=0, tiled=True)
    new_weights = (1.0 - learn_rate * decay_rate) * weights - learn_rate * back
    return (new_weights, new_momentum)


def kernel(
    rows_of,
    cols_of,
    grad_hbm,
    mom_hbm,
    weight_hbm,
    new_weight_hbm,
    new_mom_hbm,
    grad,
    mom,
    weight,
    new_mom,
    direction,
    whole,
    grams,
    mixed,
    back,
    new_weight,
    load_sem,
    store_sem,
    there_send,
    there_recv,
    gram_send,
    gram_recv,
    back_send,
    back_recv,
):
    n, t = rows_of, cols_of
    me, mine = lax.axis_index("fsdp"), lax.axis_index("tp")
    mats, rows = grad.shape[1], grad.shape[2]
    turn = 1 - 2 * (me // (n // 2)) if n % 2 == 0 else 1

    def peer(step):
        return lax.rem(me + turn * step + n, n)

    def tp_peer(step):
        return lax.rem(mine + step, t)

    def block(owner):
        return pl.ds(pl.multiple_of(owner * rows, rows), rows)

    def load(k, which):
        pairs = ((grad_hbm, grad), (mom_hbm, mom), (weight_hbm, weight))
        source, target = pairs[which]
        return pltpu.make_async_copy(source.at[:, k], target.at[:, k], load_sem.at[which, k])

    def store(k, which):
        pairs = ((new_weight, new_weight_hbm), (new_mom, new_mom_hbm))
        source, target = pairs[which]
        return pltpu.make_async_copy(source.at[:, k], target.at[:, k], store_sem.at[which, k])

    def there(k, step):
        return pltpu.make_async_remote_copy(
            src_ref=direction.at[peer(step), k],
            dst_ref=whole.at[k, block(me)],
            send_sem=there_send.at[k, step],
            recv_sem=there_recv.at[k, me],
            device_id={"fsdp": peer(step)},
            device_id_type=MESH,
        )

    def there_landed(k, step):
        return pltpu.make_async_remote_copy(
            src_ref=direction.at[peer(step), k],
            dst_ref=whole.at[k, block(peer(step))],
            send_sem=there_send.at[k, step],
            recv_sem=there_recv.at[k, peer(step)],
            device_id={"fsdp": peer(step)},
            device_id_type=MESH,
        )

    def share(k, step):
        return pltpu.make_async_remote_copy(
            src_ref=grams.at[k, mine],
            dst_ref=grams.at[k, mine],
            send_sem=gram_send.at[k, step],
            recv_sem=gram_recv.at[k, mine],
            device_id={"tp": tp_peer(step)},
            device_id_type=MESH,
        )

    def share_landed(k, step):
        return pltpu.make_async_remote_copy(
            src_ref=grams.at[k, mine],
            dst_ref=grams.at[k, tp_peer(step)],
            send_sem=gram_send.at[k, step],
            recv_sem=gram_recv.at[k, tp_peer(step)],
            device_id={"tp": tp_peer(step)},
            device_id_type=MESH,
        )

    def home(k, step):
        return pltpu.make_async_remote_copy(
            src_ref=mixed.at[k, block(peer(step))],
            dst_ref=back.at[me, k],
            send_sem=back_send.at[k, step],
            recv_sem=back_recv.at[k, me],
            device_id={"fsdp": peer(step)},
            device_id_type=MESH,
        )

    def home_landed(k, step):
        return pltpu.make_async_remote_copy(
            src_ref=mixed.at[k, block(peer(step))],
            dst_ref=back.at[peer(step), k],
            send_sem=back_send.at[k, step],
            recv_sem=back_recv.at[k, peer(step)],
            device_id={"fsdp": peer(step)},
            device_id_type=MESH,
        )

    barrier = pltpu.get_barrier_semaphore()
    for step in range(1, n):
        pl.semaphore_signal(barrier, inc=1, device_id={"fsdp": peer(step)}, device_id_type=MESH)
    for step in range(1, t):
        pl.semaphore_signal(barrier, inc=1, device_id={"tp": tp_peer(step)}, device_id_type=MESH)
    for k in range(mats):
        load(k, 0).start()
        load(k, 1).start()

    def begin(k):
        load(k, 0).wait()
        load(k, 1).wait()
        fresh = hold_rate * mom[:, k] + grad[:, k]
        new_mom[:, k] = fresh
        direction[:, k] = hold_rate * fresh + grad[:, k]
        store(k, 1).start()

    begin(0)
    pl.semaphore_wait(barrier, n + t - 2)

    def send(k, carry):
        for step in range(1, n):
            there(k, step).start()
        whole[k, block(me)] = direction[me, k]

        @pl.when(k + 1 < mats)
        def _():
            begin(k + 1)

        return carry

    lax.fori_loop(0, mats, send, 0)
    for k in range(mats):
        load(k, 2).start()

    def work(k, carry):
        for step in range(1, n):
            there_landed(k, step).wait_recv()
        grams[k, mine] = dot(whole[k], whole[k], ((1,), (1,)))
        for step in range(1, t):
            share(k, step).start()
        for step in range(1, t):
            share_landed(k, step).wait_recv()
        gram = grams[k, 0]
        for other in range(1, t):
            gram = gram + grams[k, other]
        mixed[k] = dot(mixing(gram), whole[k])
        for step in range(1, n):
            home(k, step).start()
        back[me, k] = mixed[k, block(me)]
        return carry

    lax.fori_loop(0, mats, work, 0)

    def finish(k, carry):
        load(k, 2).wait()
        for step in range(1, n):
            home_landed(k, step).wait_recv()
        new_weight[:, k] = (1.0 - learn_rate * decay_rate) * weight[:, k] - learn_rate * back[:, k]
        store(k, 0).start()
        return carry

    lax.fori_loop(0, mats, finish, 0)

    def drain(k, carry):
        for step in range(1, n):
            there(k, step).wait_send()
            home(k, step).wait_send()
        for step in range(1, t):
            share(k, step).wait_send()
        store(k, 0).wait()
        store(k, 1).wait()
        return carry

    lax.fori_loop(0, mats, drain, 0)


def shards(n, t, gradients, momentum, weights):
    total, rows, cols = gradients.shape
    if rows % 8 or cols % 128 or n < 2 or t < 2:
        return plain(gradients, momentum, weights)
    mats, side = total // n, rows * n
    cut = (n, mats, rows, cols)
    held = pltpu.VMEM(cut, jnp.float32)
    full = pltpu.VMEM((mats, side, cols), jnp.float32)
    sems = lambda *shape: pltpu.SemaphoreType.DMA(shape)
    new_weights, new_momentum = pl.pallas_call(
        functools.partial(kernel, n, t),
        out_shape=[jax.ShapeDtypeStruct(cut, jnp.float32)] * 2,
        in_specs=[pl.BlockSpec(memory_space=pl.ANY)] * 3,
        out_specs=[pl.BlockSpec(memory_space=pl.ANY)] * 2,
        scratch_shapes=[
            held,
            held,
            held,
            held,
            held,
            full,
            pltpu.VMEM((mats, t, side, side), jnp.float32),
            full,
            held,
            held,
            sems(3, mats),
            sems(2, mats),
            sems(mats, n),
            sems(mats, n),
            sems(mats, t),
            sems(mats, t),
            sems(mats, n),
            sems(mats, n),
        ],
        compiler_params=pltpu.CompilerParams(
            collective_id=0, has_side_effects=True, vmem_limit_bytes=48 * 1024 * 1024
        ),
    )(gradients.reshape(cut), momentum.reshape(cut), weights.reshape(cut))
    return (new_weights.reshape(total, rows, cols), new_momentum.reshape(total, rows, cols))


def solution(mesh):
    return jax.shard_map(
        functools.partial(shards, mesh.shape["fsdp"], mesh.shape["tp"]),
        mesh=mesh,
        in_specs=(P("copy", "fsdp", "tp"), P("copy", "fsdp", "tp"), P("copy", "fsdp", "tp")),
        out_specs=(P("copy", "fsdp", "tp"), P("copy", "fsdp", "tp")),
        check_vma=False,
    )
```

time: 187 us -> 102 us (0.55)
  blocking collectives: 106 us -> 0 us
  Pallas kernels: 0 us -> 98.2 us
  waiting for transfers between devices: 42.4 us -> 0 us
  between operations: 14.2 us -> 0.64 us
  matrix products: 12.4 us -> 0 us
  other arithmetic: 7.95 us -> 0 us
    all_to_all x2 -> x0, blocking collectives: 106 us -> none  [the longest x1 54.3 us: shards(): lax.all_to_all(direction, 'fsdp', split_axis=0, concat_axis=1, tiled=True)]
    pallas_call x0 -> x1, Pallas kernels: none -> 98.2 us  [shards(): pl.pallas_call(functools.partial(kernel, n, t), out_shape=[jax.ShapeDtype...]
    psum x1 -> x0, waiting for transfers between devices: 42.4 us -> none  [shards(): gram = lax.psum(gram, 'tp')]
    dot_general x16 -> x0, matrix products: 12.4 us -> none  [the longest x15 9.65 us: mul(): return jnp.einsum('mij,mjk->mik', a, b, precision=lax.Precision.HIGHEST)]
    add x1 -> x0, other arithmetic: 4.5 us -> none  [shards(): direction = hold_rate * new_momentum + gradients]
    unnamed x2, local copies, waits for them, and re-layouts: 0.36 us -> 2.64 us
  transfers between devices with their start and end apart: 1 -> 0, of which waited for: 1 -> 0; matrix products, arithmetic and copies ran while one was open for 0% -> 0% of each run, Pallas kernels for 0% -> 0%
where the time goes in v2:
time: 102 us; the launch traced here: 101 us
  Pallas kernels  98.2 us (96%)
  local copies, waits for them, and re-layouts  2.64 us (3%)
    pallas_call x1, Pallas kernels, shards(): pl.pallas_call(functools.partial(kernel, n, t), out_shape=[jax.ShapeDtype...  98.2 us
    unnamed x2, local copies, waits for them, and re-layouts  2.64 us

profile of v2, /device:TPU:0, one launch (start us, length us, event | category | flops | bytes accessed | tf_op | source)
XLA Modules:
  0.0 101.4 jit_solution(2097398552359326760)
XLA Ops:
  0.6 98.2 %shard_map.50 = (f32[4,4,32,1024]{3,2,1,0:T(8,128)S(1)}, f32[4,4,32,1024]{3,2,1,0:T(8,128)S(1)}) custom-call(f32[4,4,32,1024]{3,2,1,0:T(8,128)} %bitcast.7, f32[4,4,32,1024]{3,2,1,0:T(8,128)} %bitcast.8, f32[4,4,32,1024]{3,2,1,0:T(8,128)} %bitcast.9), custom_call_target="tpu_custom_call" | custom-call | tf_op jit(solution)/shard_map/pallas_call | solution.py:257
  98.8 1.3 %copy.7 = f32[16,32,1024]{2,1,0:T(8,128)} copy(f32[16,32,1024]{2,1,0:T(8,128)S(1)} %bitcast.6) | data formatting | bytes 4194304
  100.1 1.3 %copy.8 = f32[16,32,1024]{2,1,0:T(8,128)} copy(f32[16,32,1024]{2,1,0:T(8,128)S(1)} %bitcast.5) | data formatting | bytes 4194304

commit v3 on v2

--- a/solution.py
+++ b/solution.py
@@ -77,6 +77,7 @@
     new_weight,
     load_sem,
     store_sem,
+    store_weight_sem,
     there_send,
     there_recv,
     gram_send,
@@ -87,10 +88,13 @@
     n, t = rows_of, cols_of
     me, mine = lax.axis_index("fsdp"), lax.axis_index("tp")
     mats, rows = grad.shape[1], grad.shape[2]
-    turn = 1 - 2 * (me // (n // 2)) if n % 2 == 0 else 1
+    half = n // 2
+    flip = me // half
+    spot = me + flip * (n - 1 - 2 * me)
 
     def peer(step):
-        return lax.rem(me + turn * step + n, n)
+        seen = lax.rem(spot + step, half) if step < half else n - 1 - (step - half)
+        return seen + flip * (n - 1 - 2 * seen)
 
     def tp_peer(step):
         return lax.rem(mine + step, t)
@@ -103,10 +107,13 @@
         source, target = pairs[which]
         return pltpu.make_async_copy(source.at[:, k], target.at[:, k], load_sem.at[which, k])
 
-    def store(k, which):
-        pairs = ((new_weight, new_weight_hbm), (new_mom, new_mom_hbm))
-        source, target = pairs[which]
-        return pltpu.make_async_copy(source.at[:, k], target.at[:, k], store_sem.at[which, k])
+    def store_mom(k):
+        return pltpu.make_async_copy(new_mom.at[:, k], new_mom_hbm.at[:, k], store_sem.at[k])
+
+    def store_weight(k, owner):
+        return pltpu.make_async_copy(
+            new_weight.at[owner, k], new_weight_hbm.at[owner, k], store_weight_sem.at[owner, k]
+        )
 
     def there(k, step):
         return pltpu.make_async_remote_copy(
@@ -183,7 +190,7 @@
         fresh = hold_rate * mom[:, k] + grad[:, k]
         new_mom[:, k] = fresh
         direction[:, k] = hold_rate * fresh + grad[:, k]
-        store(k, 1).start()
+        store_mom(k).start()
 
     begin(0)
     pl.semaphore_wait(barrier, n + t - 2)
@@ -222,12 +229,18 @@
 
     lax.fori_loop(0, mats, work, 0)
 
+    def update(k, owner):
+        new_weight[owner, k] = (1.0 - learn_rate * decay_rate) * weight[
+            owner, k
+        ] - learn_rate * back[owner, k]
+        store_weight(k, owner).start()
+
     def finish(k, carry):
         load(k, 2).wait()
+        update(k, me)
         for step in range(1, n):
             home_landed(k, step).wait_recv()
-        new_weight[:, k] = (1.0 - learn_rate * decay_rate) * weight[:, k] - learn_rate * back[:, k]
-        store(k, 0).start()
+            update(k, peer(step))
         return carry
 
     lax.fori_loop(0, mats, finish, 0)
@@ -238,16 +251,31 @@
             home(k, step).wait_send()
         for step in range(1, t):
             share(k, step).wait_send()
-        store(k, 0).wait()
-        store(k, 1).wait()
+        for owner in range(n):
+            store_weight(k, owner).wait()
+        store_mom(k).wait()
         return carry
 
     lax.fori_loop(0, mats, drain, 0)
+
+
+def write_kernel(new_weight, new_mom, new_weight_hbm, new_mom_hbm, sem):
+    copies = [
+        pltpu.make_async_copy(source.at[i], target.at[i], sem.at[which, i])
+        for which, (source, target) in enumerate(
+            ((new_mom, new_mom_hbm), (new_weight, new_weight_hbm))
+        )
+        for i in range(source.shape[0])
+    ]
+    for copy in copies:
+        copy.start()
+    for copy in copies:
+        copy.wait()
 
 
 def shards(n, t, gradients, momentum, weights):
     total, rows, cols = gradients.shape
-    if rows % 8 or cols % 128 or n < 2 or t < 2:
+    if rows % 8 or cols % 128 or n % 2 or t < 2:
         return plain(gradients, momentum, weights)
     mats, side = total // n, rows * n
     cut = (n, mats, rows, cols)
@@ -271,7 +299,8 @@
             held,
             held,
             sems(3, mats),
-            sems(2, mats),
+            sems(mats),
+            sems(n, mats),
             sems(mats, n),
             sems(mats, n),
             sems(mats, t),
@@ -283,6 +312,14 @@
             collective_id=0, has_side_effects=True, vmem_limit_bytes=48 * 1024 * 1024
         ),
     )(gradients.reshape(cut), momentum.reshape(cut), weights.reshape(cut))
+    new_weights, new_momentum = pl.pallas_call(
+        write_kernel,
+        out_shape=[jax.ShapeDtypeStruct(cut, jnp.float32)] * 2,
+        in_specs=[pl.BlockSpec(memory_space=pl.ANY)] * 2,
+        out_specs=[pl.BlockSpec(memory_space=pltpu.HBM)] * 2,
+        scratch_shapes=[sems(2, n)],
+        compiler_params=pltpu.CompilerParams(vmem_limit_bytes=1024 * 1024),
+    )(new_weights, new_momentum)
     return (new_weights.reshape(total, rows, cols), new_momentum.reshape(total, rows, cols))
 
 

time: 102 us -> 99.5 us (0.975)
  local copies, waits for them, and re-layouts: 2.64 us -> 0 us
    unnamed x2 -> x0, local copies, waits for them, and re-layouts: 2.64 us -> none
    pallas_call x0 -> x1, Pallas kernels: none -> 2.07 us  [shards(): pl.pallas_call(write_kernel, out_shape=[jax.ShapeDtypeStruct(cut, jnp.flo...]
    pallas_call x1, Pallas kernels: 98.2 us -> 96.6 us  [shards(): pl.pallas_call(functools.partial(kernel, n, t), out_shape=[jax.ShapeDtype...]
where the time goes in v3:
time: 99.5 us; the launch traced here: 99.3 us
  Pallas kernels  98.7 us (99%)
    pallas_call x1, Pallas kernels, shards(): pl.pallas_call(functools.partial(kernel, n, t), out_shape=[jax.ShapeDtype...  96.6 us
    pallas_call x1, Pallas kernels, shards(): pl.pallas_call(write_kernel, out_shape=[jax.ShapeDtypeStruct(cut, jnp.flo...  2.07 us

profile of v3, /device:TPU:0, one launch (start us, length us, event | category | flops | bytes accessed | tf_op | source)
XLA Modules:
  0.0 99.3 jit_solution(3141777490285940554)
XLA Ops:
  0.6 96.6 %shard_map.50 = (f32[4,4,32,1024]{3,2,1,0:T(8,128)S(1)}, f32[4,4,32,1024]{3,2,1,0:T(8,128)S(1)}) custom-call(f32[4,4,32,1024]{3,2,1,0:T(8,128)} %bitcast.5, f32[4,4,32,1024]{3,2,1,0:T(8,128)} %bitcast.6, f32[4,4,32,1024]{3,2,1,0:T(8,128)} %bitcast.7), custom_call_target="tpu_custom_call" | custom-call | tf_op jit(solution)/shard_map/pallas_call | solution.py:285
  97.3 2.1 %shard_map.51 = (f32[4,4,32,1024]{3,2,1,0:T(8,128)}, f32[4,4,32,1024]{3,2,1,0:T(8,128)}) custom-call(f32[4,4,32,1024]{3,2,1,0:T(8,128)S(1)} %get-tuple-element.6.new_weight, f32[4,4,32,1024]{3,2,1,0:T(8,128)S(1)} %get-tuple-element.7.new_mom), custom_call_target="tpu_custom_call" | custom-call | tf_op jit(solution)/shard_map/pallas_call | solution.py:315
